TPU v7x, 32 devices: a whole 2x2x4 slice. The times are simulated.
32 devices in a mesh: gx: 2 (over core), gy: 4 (over y, x), ma: 4 (over z).
Axes of the slice: x: 2, y: 2, z: 4, core: 2. Of those that a mesh axis runs over, the one named last changes fastest.
Arguments:
- object_field: float32 [2, 256, 1024], P(None, 'gx', 'gy'), may hold values from -5 to 5
- probe_modes: float32 [8, 2, 256, 256], P('ma'), may hold values from -1.5 to 1.5
- measured: float32 [2, 4, 2, 256, 256], P('gx', 'gy'), may hold values from 0.1 to 4
- positions: int32 [2, 4, 2, 2], P('gx', 'gy'), may hold values from 0 to 255, as said below
- slot_counts: int32 [2, 4], P('gx', 'gy'), may hold values from 1 to 2, as said below
Outputs:
- updated_object: float32 [2, 256, 1024], P(None, 'gx', 'gy')
Inputs may be any that keep to these rules, and one draw needn't show every extreme that they name: positions[a, b, s] holds a row 0 to 127 and a column 0 to 255 of tile (a, b); slots s >= slot_counts[a, b] are unused. `slot_counts`: some tile uses all 2 slots.
All inputs are finite; a program needn't handle non-finite values.
Results may differ from a plain program's by a relative error of at most 0.0023.
Values sent between devices are 32-bit elements; how exact they have to be, the bound alone decides.
A program may use at most 64 MiB of HBM per device.

v0:
```python
import math
import jax
import jax.numpy as jnp
import numpy as np
from jax import lax
from jax.sharding import PartitionSpec as P

OUTER = 2
DAMPING = 1.0


def dft_tables(patch_width):
    ladder = np.arange(patch_width)
    angles = ladder[:, None] * ladder[None, :] % patch_width * (2.0 * math.pi / patch_width)
    factor = 1.0 / math.sqrt(patch_width)
    real_part = np.cos(angles) * factor
    imag_part = -np.sin(angles) * factor
    table_one = np.block([[real_part, -imag_part], [imag_part, real_part]])
    table_two = np.block([[real_part, imag_part], [-imag_part, real_part]])
    return (jnp.asarray(table_one, jnp.bfloat16), jnp.asarray(table_two, jnp.bfloat16))


def shift_pair(low_part, high_part, axis):
    count = lax.axis_size(axis)
    forward = [(i, i + 1) for i in range(count - 1)]
    backward = [(target, source) for source, target in forward]
    return (lax.ppermute(high_part, axis, forward), lax.ppermute(low_part, axis, backward))


def widen(block, axis, dim, width):
    size = block.shape[dim]
    low, high = shift_pair(
        lax.slice_in_dim(block, 0, width, axis=dim),
        lax.slice_in_dim(block, size - width, None, axis=dim),
        axis,
    )
    return jnp.concatenate([low, block, high], axis=dim)


def fold(block, axis, dim, width):
    size = block.shape[dim]
    low, high = shift_pair(
        lax.slice_in_dim(block, 0, width, axis=dim),
        lax.slice_in_dim(block, size - width, None, axis=dim),
        axis,
    )
    middle = lax.slice_in_dim(block, width, size - width, axis=dim)
    pads = [(0, 0)] * 3
    pads[dim] = (0, size - 3 * width)
    first = jnp.pad(low, pads)
    pads[dim] = (size - 3 * width, 0)
    return middle + first + jnp.pad(high, pads)


def shards(object_field, probe_shard, measured, positions, slot_counts):
    patch = probe_shard.shape[-1]
    rim = patch // 2
    rows, cols = object_field.shape[1:]
    slots = measured.shape[2]
    share = patch // lax.axis_size("ma")
    first = lax.axis_index("ma") * share
    table_one, table_two = dft_tables(patch)
    left_one = lax.dynamic_slice_in_dim(table_one.reshape(2, patch, 2, patch), first, share, 1)
    right_two = table_two.reshape(2, patch, 2 * patch)
    left_two = lax.dynamic_slice_in_dim(table_two.reshape(2, patch, 2, patch), first, share, 3)
    targets = lax.dynamic_slice_in_dim(measured[0, 0], first, share, 1)
    centres = positions[0, 0]
    live = (jnp.arange(slots, dtype=jnp.int32) < slot_counts[0, 0]).astype(jnp.float32)
    live = live[:, None, None]
    anchor = jnp.zeros((), jnp.int32)
    probes = lax.all_gather(probe_shard, "ma", axis=0, tiled=True)
    modes = probes.shape[0]
    probe_real, probe_imag = (probes[None, :, 0], probes[None, :, 1])

    def spectra_of(tile):
        padded = widen(widen(tile, "gy", 2, rim), "gx", 1, rim)
        windows = jnp.stack(
            [
                lax.dynamic_slice(padded, (anchor, centres[s, 0], centres[s, 1]), (2, patch, patch))
                for s in range(slots)
            ]
        )
        real, imag = (windows[:, None, 0], windows[:, None, 1])
        waves = jnp.stack(
            [probe_real * real - probe_imag * imag, probe_real * imag + probe_imag * real], 2
        ).astype(jnp.bfloat16)
        halfway = jnp.einsum(
            "pqci,smcik->smpqk", left_one, waves, preferred_element_type=jnp.float32
        ).astype(jnp.bfloat16)
        return jnp.einsum("smcik,ckl->smil", halfway, right_two, preferred_element_type=jnp.float32)

    def mode_sum(first_spectra, second_spectra):
        product = first_spectra * second_spectra
        return jnp.sum(product[..., :patch] + product[..., patch:], axis=1)

    def project(weights, spectra):
        doubled = jnp.concatenate([weights, weights], -1)[:, None]
        scaled = (2.0 * spectra * doubled).astype(jnp.bfloat16)
        turned = jnp.einsum(
            "smik,kl->smil", scaled, table_one, preferred_element_type=jnp.float32
        ).astype(jnp.bfloat16)
        back = jnp.einsum(
            "pqci,smicl->smpql",
            left_two,
            turned.reshape(slots, modes, share, 2, patch),
            preferred_element_type=jnp.float32,
        )
        real = jnp.sum(probe_real * back[:, :, 0] + probe_imag * back[:, :, 1], axis=1)
        imag = jnp.sum(probe_real * back[:, :, 1] - probe_imag * back[:, :, 0], axis=1)
        pieces = jnp.stack([real, imag], 1)
        canvas = jnp.zeros((2, rows + patch, cols + patch), jnp.float32)
        room = jnp.pad(pieces, ((0, 0), (0, 0), (rows, rows), (cols, cols)))
        for s in range(slots):
            canvas = canvas + lax.dynamic_slice(
                room[s], (anchor, rows - centres[s, 0], cols - centres[s, 1]), canvas.shape
            )
        return lax.psum(fold(fold(canvas, "gx", 1, rim), "gy", 2, rim), "ma")

    current = object_field
    spectra = spectra_of(current)
    for outer_step in range(OUTER):
        misfit = live * (mode_sum(spectra, spectra) - targets)
        direction = -project(misfit, spectra)
        moved = spectra_of(direction)
        change = 2.0 * live * mode_sum(spectra, moved)
        sums = jnp.stack(
            [jnp.sum(direction * direction) / lax.axis_size("ma"), jnp.sum(change * change)]
        )
        sums = lax.psum(sums, ("gx", "gy", "ma"))
        step_size = sums[0] / (DAMPING * sums[0] + sums[1])
        current = current + step_size * direction
        if outer_step + 1 < OUTER:
            spectra = spectra + step_size * moved
    return current


def solution(mesh):
    return jax.shard_map(
        shards,
        mesh=mesh,
        in_specs=(
            P(None, "gx", "gy"),
            P("ma", None, None, None),
            P("gx", "gy", None, None, None),
            P("gx", "gy", None, None),
            P("gx", "gy"),
        ),
        out_specs=P(None, "gx", "gy"),
        check_vma=False,
    )
```

profile of v0, /device:TPU:0, one launch (start us, length us, event | category | flops | bytes accessed | tf_op | source)
XLA Modules:
  0.0 401.5 jit_solution(1194735594641044020)
XLA Ops:
  8.3 4.9 %collective-permute-start = (f32[2,128,128]{2,1,0:T(8,128)S(1)}, f32[2,128,128]{2,1,0:T(8,128)S(1)}, u32[]{:S(2)}, u32[]{:S(2)}) collective-permute-start(f32[2,128,128]{2,1,0:T(8,128)S(1)} %get-tuple-element.52), channel_id=1, source_target_pairs={{0,4},{4,8},{8,12},{1,5},{5,9},{9,13},{2,6},{6,10},{10,14},{3,7},{... | collective-permute-start | bytes 393224 | tf_op jit(solution)/shard_map/ppermute | solution.py:27
  13.2 1.3 collective-permute-start.1
  14.5 1.4 collective-permute-done
  16.9 3.8 collective-permute-done.1
  20.7 1.3 collective-permute-start.2
  22.0 1.3 collective-permute-start.3
  37.8 54.5 %all-gather.2.cloned.1.call-done = f32[8,2,256,256]{3,2,1,0:T(8,128)} async-done(((f32[2,2,256,256]{3,2,1,0:T(8,128)}), f32[8,2,256,256]{3,2,1,0:T(8,128)}) %all-gather.2.cloned.1.call-update) | async-done | bytes 4194320 | tf_op jit(solution)/shard_map/all_gather | solution.py:71
  92.4 4.0 slice_bitcast_fusion.5
  96.4 1.8 copy.42
  98.2 2.9 copy.45
  101.1 4.8 %subtract_convert_fusion.2 = (bf16[2,8,1,256,256]{4,3,2,1,0:T(8,128)(2,1)}, bf16[2,8,1,256,256]{4,3,2,1,0:T(8,128)(2,1)}) fusion(f32[2,256,256]{2,1,0:T(8,128)S(1)} %get-tuple-element.38, f32[8,256,256]{2,1,0:T(8,128)} %get-tuple-element.22, f32[2,256,256]{2,1,0:T(8,128)S(1)} %get-tuple-element.37, f32[8,256,256]{2,1,0:T(8,128)S(1)} %get-tuple-element.21), kind=kLoop, calls=%fused_computation.41 | loop fusion | flops 8388608 | bytes 9437184 | tf_op jit(solution)/shard_map/convert.4
  105.8 5.6 %bitcast_multiply_fusion.4 = (f32[2,8,64,512]{3,2,1,0:T(8,128)}, f32[2,8,64,512,1]{3,2,4,1,0:T(8,128)}) fusion(bf16[2,256,512,1,1]{2,1,0,4,3:T(8,128)(2,1)} %constant.64, bf16[2,8,1,256,256]{4,3,2,1,0:T(8,128)(2,1)} %get-tuple-element.20, bf16[2,8,1,256,256]{4,3,2,1,0:T(8,128)(2,1)} %get-tuple-element.19, bf16[2,256,2,256]{3,1,2,0:T(8,128)(2,1)} %constant.61, ...), kind=kOutput, calls=%fused_computation.53 | convolution fusion | flops 1083179008 | bytes 9043972 | tf_op jit(solution)/shard_map/smcik,ckl->smil/dot_general | solution.py:90
  111.4 1.8 fusion.27
  114.3 1.8 convolution_convert_fusion.1
  116.1 1.3 reshape.91
  117.5 2.3 convolution_bitcast_fusion.1
  119.8 1.6 add_reduce_fusion.1
  124.0 1.6 collective-permute-start.4
  125.6 1.3 collective-permute-start.5
  127.1 2.3 collective-permute-done.5
  129.6 3.4 collective-permute-start.6
  132.9 1.3 collective-permute-start.7
  134.2 1.7 collective-permute-done.6
  136.0 4.7 %collective-permute-done.7 = f32[2,128,128]{1,2,0:T(8,128)S(1)} collective-permute-done((f32[2,128,128]{1,2,0:T(8,128)S(1)}, f32[2,128,128]{1,2,0:T(8,128)S(1)}, u32[]{:S(2)}, u32[]{:S(2)}) %collective-permute-start.7) | collective-permute-done | bytes 131104 | tf_op jit(solution)/shard_map/ppermute | solution.py:27
  141.5 33.7 %all-reduce.9.cloned.1.call-done = f32[2,128,256]{1,2,0:T(8,128)} async-done(((f32[2,128,256]{1,2,0:T(8,128)}), f32[2,128,256]{1,2,0:T(8,128)}) %all-reduce.9.cloned.1.call-update) | async-done | bytes 262160 | tf_op jit(solution)/shard_map/psum | solution.py:117
  175.3 1.7 multiply_reduce_fusion.1
  177.0 3.4 collective-permute-start.8
  180.4 1.3 collective-permute-start.9
  181.7 1.2 collective-permute-done.8
  182.9 4.4 %collective-permute-done.9 = f32[2,128,128]{1,2,0:T(8,128)S(1)} collective-permute-done((f32[2,128,128]{1,2,0:T(8,128)S(1)}, f32[2,128,128]{1,2,0:T(8,128)S(1)}, u32[]{:S(2)}, u32[]{:S(2)}) %collective-permute-start.9) | collective-permute-done | bytes 131104 | tf_op jit(solution)/shard_map/ppermute | solution.py:27
  187.9 1.3 collective-permute-start.10
  189.3 1.5 collective-permute-start.11
  191.4 1.7 collective-permute-done.11
  196.0 1.3 fusion.34
  197.8 3.4 subtract_convert_fusion.1
  201.1 6.2 %bitcast_multiply_fusion.2 = (f32[2,8,64,512]{3,2,1,0:T(8,128)}, f32[2,8,64,512,1]{3,2,4,1,0:T(8,128)}) fusion(f32[2,8,64,512,1]{3,2,4,1,0:T(8,128)} %get-tuple-element.62, bf16[2,256,512,1,1]{2,1,0,4,3:T(8,128)(2,1)S(1)} %copy-done.13, bf16[2,8,1,256,256]{4,3,2,1,0:T(8,128)(2,1)} %get-tuple-element.18, bf16[2,8,1,256,256]{4,3,2,1,0:T(8,128)(2,1)} %get-tuple-element.17, ...), kind=kOutput, calls=%fused_computation.49 | convolution fusion | flops 1083179008 | bytes 11141124 | tf_op jit(solution)/shard_map/smcik,ckl->smil/dot_general | solution.py:90
  207.3 1.7 fusion.26
  210.4 39.8 %psum.29 = f32[2]{0:T(128)S(1)} all-reduce(f32[2]{0:T(128)S(1)} %pad_maximum_fusion.8), channel_id=1, replica_groups=mesh['gx'=2,'gy'=4,'ma'=4] {'gx','gy','ma'}, use_global_device_ids=true, to_apply=%region_7.8 | all-reduce | flops 2 | bytes 16 | tf_op jit(solution)/shard_map/psum | solution.py:129
  252.5 3.0 fusion.72
  255.7 1.5 fusion.57
  258.0 2.3 convolution_bitcast_fusion
  260.4 1.6 add_reduce_fusion
  264.5 1.3 collective-permute-start.12
  265.8 1.3 collective-permute-start.13
  267.3 2.3 collective-permute-done.13
  269.8 4.2 %collective-permute-start.14 = (f32[2,128,128]{1,2,0:T(8,128)S(1)}, f32[2,128,128]{1,2,0:T(8,128)S(1)}, u32[]{:S(2)}, u32[]{:S(2)}) collective-permute-start(f32[2,128,128]{1,2,0:T(8,128)S(1)} %get-tuple-element.39), channel_id=1, source_target_pairs={{0,4},{4,8},{8,12},{1,5},{5,9},{9,13},{2,6},{6,10},{10,14},{3,7},{... | collective-permute-start | bytes 393224 | tf_op jit(solution)/shard_map/ppermute | solution.py:27
  274.0 1.3 collective-permute-start.15
  275.3 1.7 collective-permute-done.14
  277.0 4.7 %collective-permute-done.15 = f32[2,128,128]{1,2,0:T(8,128)S(1)} collective-permute-done((f32[2,128,128]{1,2,0:T(8,128)S(1)}, f32[2,128,128]{1,2,0:T(8,128)S(1)}, u32[]{:S(2)}, u32[]{:S(2)}) %collective-permute-start.15) | collective-permute-done | bytes 131104 | tf_op jit(solution)/shard_map/ppermute | solution.py:27
  282.5 34.8 %all-reduce.11.cloned.1.call-done = f32[2,128,256]{1,2,0:T(8,128)} async-done(((f32[2,128,256]{1,2,0:T(8,128)}), f32[2,128,256]{1,2,0:T(8,128)}) %all-reduce.11.cloned.1.call-update) | async-done | bytes 262160 | tf_op jit(solution)/shard_map/psum | solution.py:117
  317.3 1.6 multiply_reduce_fusion
  318.9 3.4 collective-permute-start.16
  322.3 1.3 collective-permute-start.17
  323.6 1.2 collective-permute-done.16
  324.8 4.4 %collective-permute-done.17 = f32[2,128,128]{1,2,0:T(8,128)S(1)} collective-permute-done((f32[2,128,128]{1,2,0:T(8,128)S(1)}, f32[2,128,128]{1,2,0:T(8,128)S(1)}, u32[]{:S(2)}, u32[]{:S(2)}) %collective-permute-start.17) | collective-permute-done | bytes 131104 | tf_op jit(solution)/shard_map/ppermute | solution.py:27
  329.9 1.3 collective-permute-start.18
  331.2 1.5 collective-permute-start.19
  333.3 1.9 collective-permute-done.19
  335.1 1.2 pad_maximum_fusion.2
  337.9 1.3 fusion.32
  339.6 3.3 subtract_convert_fusion
  342.9 5.5 %bitcast_multiply_fusion = f32[2,8,64,512]{3,2,1,0:T(8,128)} fusion(f32[2,8,64,512]{3,2,1,0:T(8,128)} %copy-done.7, bf16[2,256,512,1,1]{2,1,0,4,3:T(8,128)(2,1)S(1)} %copy-done.14, bf16[2,8,1,256,256]{4,3,2,1,0:T(8,128)(2,1)} %get-tuple-element.16, bf16[2,8,1,256,256]{4,3,2,1,0:T(8,128)(2,1)} %get-tuple-element.15, bf16[2,256,2,256]{3,1,2,0:T(8,128)(2,1)} %constant.61, ...), kind=kOutput, calls=%fused_computation.46 | convolution fusion | flops 1083179008 | bytes 9043972 | tf_op jit(solution)/shard_map/smcik,ckl->smil/dot_general | solution.py:90
  348.4 1.8 fusion.24
  351.8 39.8 %psum.31 = f32[2]{0:T(128)S(1)} all-reduce(f32[2]{0:T(128)S(1)} %pad_maximum_fusion.9), channel_id=1, replica_groups=mesh['gx'=2,'gy'=4,'ma'=4] {'gx','gy','ma'}, use_global_device_ids=true, to_apply=%region_15.16 | all-reduce | flops 2 | bytes 16 | tf_op jit(solution)/shard_map/psum | solution.py:129
  (97 shorter events, 24.9 us)
Async XLA Ops:
  6.5 16.8 %copy-start.17 = (s32[1,1,2,2]{3,2,1,0:T(2,128)S(1)}, s32[1,1,2,2]{3,2,1,0:T(2,128)}, u32[]{:S(2)}) copy-start(s32[1,1,2,2]{3,2,1,0:T(2,128)} %param.10) | copy-start | bytes 52
  6.5 85.9 %all-gather.2.cloned.1.call-start = ((), (), s32[]{:S(2)}) async-start(), calls=%async_computation | async-start | bytes 5242880 | tf_op jit(solution)/shard_map/all_gather | solution.py:71
  7.3 168.0 %all-reduce.9.cloned.1.call-start = ((), (), s32[]{:S(2)}) async-start(), calls=%async_computation.1 | async-start | bytes 524288 | tf_op jit(solution)/shard_map/psum | solution.py:117
  8.3 7.6 %collective-permute-start = (f32[2,128,128]{2,1,0:T(8,128)S(1)}, f32[2,128,128]{2,1,0:T(8,128)S(1)}, u32[]{:S(2)}, u32[]{:S(2)}) collective-permute-start(f32[2,128,128]{2,1,0:T(8,128)S(1)} %get-tuple-element.52), channel_id=1, source_target_pairs={{0,4},{4,8},{8,12},{1,5},{5,9},{9,13},{2,6},{6,10},{10,14},{3,7},{... | collective-permute-start | bytes 393224 | tf_op jit(solution)/shard_map/ppermute | solution.py:27
  13.2 7.5 %collective-permute-start.1 = (f32[2,128,128]{2,1,0:T(8,128)S(1)}, f32[2,128,128]{2,1,0:T(8,128)S(1)}, u32[]{:S(2)}, u32[]{:S(2)}) collective-permute-start(f32[2,128,128]{2,1,0:T(8,128)S(1)} %get-tuple-element.51), channel_id=1, source_target_pairs={{4,0},{8,4},{12,8},{5,1},{9,5},{13,9},{6,2},{10,6},{14,10},{7,3},{... | collective-permute-start | bytes 393224 | tf_op jit(solution)/shard_map/ppermute | solution.py:27
  20.7 16.6 %collective-permute-start.2 = (f32[2,128,512]{2,1,0:T(8,128)S(1)}, f32[2,128,512]{2,1,0:T(8,128)S(1)}, u32[]{:S(2)}, u32[]{:S(2)}) collective-permute-start(f32[2,128,512]{2,1,0:T(8,128)S(1)} %constant_dynamic-update-slice_fusion), channel_id=1, source_target_pairs={{0,16},{1,17},{2,18},{3,19},{4,20},{5,21},{6,22},{7,23},{8,24},{9,... | collective-permute-start | bytes 1572872 | tf_op jit(solution)/shard_map/ppermute | solution.py:27
  22.0 15.2 %collective-permute-start.3 = (f32[2,128,512]{2,1,0:T(8,128)S(1)}, f32[2,128,512]{2,1,0:T(8,128)S(1)}, u32[]{:S(2)}, u32[]{:S(2)}) collective-permute-start(f32[2,128,512]{2,1,0:T(8,128)S(1)} %constant_dynamic-update-slice_fusion), channel_id=1, source_target_pairs={{16,0},{17,1},{18,2},{19,3},{20,4},{21,5},{22,6},{23,7},{24,8},{25... | collective-permute-start | bytes 1572872 | tf_op jit(solution)/shard_map/ppermute | solution.py:27
  111.4 2.9 copy-start.6
  111.4 2.9 copy-start.9
  117.5 2.4 copy-start.2
  117.5 2.4 copy-start.4
  124.0 3.1 collective-permute-start.4
  125.6 3.8 collective-permute-start.5
  129.6 6.4 %collective-permute-start.6 = (f32[2,128,128]{1,2,0:T(8,128)S(1)}, f32[2,128,128]{1,2,0:T(8,128)S(1)}, u32[]{:S(2)}, u32[]{:S(2)}) collective-permute-start(f32[2,128,128]{1,2,0:T(8,128)S(1)} %get-tuple-element.41), channel_id=1, source_target_pairs={{0,4},{4,8},{8,12},{1,5},{5,9},{9,13},{2,6},{6,10},{10,14},{3,7},{... | collective-permute-start | bytes 393224 | tf_op jit(solution)/shard_map/ppermute | solution.py:27
  132.9 7.8 %collective-permute-start.7 = (f32[2,128,128]{1,2,0:T(8,128)S(1)}, f32[2,128,128]{1,2,0:T(8,128)S(1)}, u32[]{:S(2)}, u32[]{:S(2)}) collective-permute-start(f32[2,128,128]{1,2,0:T(8,128)S(1)} %get-tuple-element.42), channel_id=1, source_target_pairs={{4,0},{8,4},{12,8},{5,1},{9,5},{13,9},{6,2},{10,6},{14,10},{7,3},{... | collective-permute-start | bytes 393224 | tf_op jit(solution)/shard_map/ppermute | solution.py:27
  141.5 175.8 %all-reduce.11.cloned.1.call-start = ((), (), s32[]{:S(2)}) async-start(), calls=%async_computation.2 | async-start | bytes 524288 | tf_op jit(solution)/shard_map/psum | solution.py:117
  177.0 5.9 %collective-permute-start.8 = (f32[2,128,128]{1,2,0:T(8,128)S(1)}, f32[2,128,128]{1,2,0:T(8,128)S(1)}, u32[]{:S(2)}, u32[]{:S(2)}) collective-permute-start(f32[2,128,128]{1,2,0:T(8,128)S(1)} %get-tuple-element.49), channel_id=1, source_target_pairs={{0,4},{4,8},{8,12},{1,5},{5,9},{9,13},{2,6},{6,10},{10,14},{3,7},{... | collective-permute-start | bytes 393224 | tf_op jit(solution)/shard_map/ppermute | solution.py:27
  180.4 6.9 %collective-permute-start.9 = (f32[2,128,128]{1,2,0:T(8,128)S(1)}, f32[2,128,128]{1,2,0:T(8,128)S(1)}, u32[]{:S(2)}, u32[]{:S(2)}) collective-permute-start(f32[2,128,128]{1,2,0:T(8,128)S(1)} %get-tuple-element.50), channel_id=1, source_target_pairs={{4,0},{8,4},{12,8},{5,1},{9,5},{13,9},{6,2},{10,6},{14,10},{7,3},{... | collective-permute-start | bytes 393224 | tf_op jit(solution)/shard_map/ppermute | solution.py:27
  187.2 0.7 copy-start.15
  187.9 3.5 collective-permute-start.10
  189.3 3.9 collective-permute-start.11
  196.0 1.7 copy-start
  197.8 3.4 copy-start.13
  255.5 2.5 copy-start.7
  255.5 1.7 copy-start.10
  258.0 2.4 copy-start.3
  258.0 2.4 copy-start.5
  264.5 2.8 collective-permute-start.12
  265.8 3.8 collective-permute-start.13
  269.8 7.2 %collective-permute-start.14 = (f32[2,128,128]{1,2,0:T(8,128)S(1)}, f32[2,128,128]{1,2,0:T(8,128)S(1)}, u32[]{:S(2)}, u32[]{:S(2)}) collective-permute-start(f32[2,128,128]{1,2,0:T(8,128)S(1)} %get-tuple-element.39), channel_id=1, source_target_pairs={{0,4},{4,8},{8,12},{1,5},{5,9},{9,13},{2,6},{6,10},{10,14},{3,7},{... | collective-permute-start | bytes 393224 | tf_op jit(solution)/shard_map/ppermute | solution.py:27
  274.0 7.8 %collective-permute-start.15 = (f32[2,128,128]{1,2,0:T(8,128)S(1)}, f32[2,128,128]{1,2,0:T(8,128)S(1)}, u32[]{:S(2)}, u32[]{:S(2)}) collective-permute-start(f32[2,128,128]{1,2,0:T(8,128)S(1)} %get-tuple-element.40), channel_id=1, source_target_pairs={{4,0},{8,4},{12,8},{5,1},{9,5},{13,9},{6,2},{10,6},{14,10},{7,3},{... | collective-permute-start | bytes 393224 | tf_op jit(solution)/shard_map/ppermute | solution.py:27
  318.9 5.9 %collective-permute-start.16 = (f32[2,128,128]{1,2,0:T(8,128)S(1)}, f32[2,128,128]{1,2,0:T(8,128)S(1)}, u32[]{:S(2)}, u32[]{:S(2)}) collective-permute-start(f32[2,128,128]{1,2,0:T(8,128)S(1)} %get-tuple-element.45), channel_id=1, source_target_pairs={{0,4},{4,8},{8,12},{1,5},{5,9},{9,13},{2,6},{6,10},{10,14},{3,7},{... | collective-permute-start | bytes 393224 | tf_op jit(solution)/shard_map/ppermute | solution.py:27
  322.3 6.9 %collective-permute-start.17 = (f32[2,128,128]{1,2,0:T(8,128)S(1)}, f32[2,128,128]{1,2,0:T(8,128)S(1)}, u32[]{:S(2)}, u32[]{:S(2)}) collective-permute-start(f32[2,128,128]{1,2,0:T(8,128)S(1)} %get-tuple-element.46), channel_id=1, source_target_pairs={{4,0},{8,4},{12,8},{5,1},{9,5},{13,9},{6,2},{10,6},{14,10},{7,3},{... | collective-permute-start | bytes 393224 | tf_op jit(solution)/shard_map/ppermute | solution.py:27
  329.2 0.7 copy-start.16
  329.9 3.4 collective-permute-start.18
  331.2 3.9 collective-permute-start.19
  337.9 1.7 copy-start.1
  339.6 3.3 copy-start.14
  348.4 3.2 copy-start.8
  348.4 45.6 %copy-start.11 = (f32[2,128,256]{1,2,0:T(8,128)S(1)}, f32[2,128,256]{1,2,0:T(8,128)}, u32[]{:S(2)}) copy-start(f32[2,128,256]{1,2,0:T(8,128)} %all-reduce.9.cloned.1.call-done) | copy-start | bytes 786436
  348.4 45.6 %copy-start.12 = (f32[2,128,256]{1,2,0:T(8,128)S(1)}, f32[2,128,256]{1,2,0:T(8,128)}, u32[]{:S(2)}) copy-start(f32[2,128,256]{1,2,0:T(8,128)} %all-reduce.11.cloned.1.call-done) | copy-start | bytes 786436
Sparse Core Ops, SparseCore 0:
  8.9 83.4 all-gather.1
  141.6 33.6 all-reduce.8
  282.6 34.6 all-reduce.10
where the time goes:
time: 403 us; the launch traced here: 402 us
  waiting for transfers between devices  162 us (40%)
  blocking collectives  79.6 us (20%)
  other arithmetic  42 us (10%)
  starting transfers between devices  39.5 us (10%)
  between operations  31.9 us (8%)
  matrix products  24.5 us (6%)
  local copies, waits for them, and re-layouts  22.3 us (6%)
    psum x2, blocking collectives, shards(): sums = lax.psum(sums, ('gx', 'gy', 'ma'))  79.6 us
    psum x2, waiting for transfers between devices, project(): return lax.psum(fold(fold(canvas, 'gx', 1, rim), 'gy', 2, rim), 'ma')  68.5 us
    all_gather x1, waiting for transfers between devices, shards(): probes = lax.all_gather(probe_shard, 'ma', axis=0, tiled=True)  54.5 us
    ppermute x10, waiting for transfers between devices, shift_pair(): lax.ppermute(low_part, axis, backward)  30.2 us
    ppermute x10, starting transfers between devices, shift_pair(): lax.ppermute(high_part, axis, forward)  26.1 us
    dot_general x3, matrix products, spectra_of(): jnp.einsum('smcik,ckl->smil', halfway, right_two, preferred_element_type=...  17.3 us
    ppermute x10, starting transfers between devices, shift_pair(): lax.ppermute(low_part, axis, backward)  13.3 us
    another operation x3, other arithmetic  11.4 us
  transfers between devices with their start and end apart: 23, of which 19 were waited for; matrix products, arithmetic and copies ran while one was open for 1% of the time, Pallas kernels for 0%

commit v1 on v0

--- a/solution.py
+++ b/solution.py
@@ -114,7 +114,7 @@
             canvas = canvas + lax.dynamic_slice(
                 room[s], (anchor, rows - centres[s, 0], cols - centres[s, 1]), canvas.shape
             )
-        return lax.psum(fold(fold(canvas, "gx", 1, rim), "gy", 2, rim), "ma")
+        return lax.all_gather(fold(fold(canvas, "gx", 1, rim), "gy", 2, rim), "ma").sum(axis=0)
 
     current = object_field
     spectra = spectra_of(current)

time: 403 us -> 386 us (0.958)
  waiting for transfers between devices: 162 us -> 142 us
  starting transfers between devices: 39.5 us -> 47.5 us
    psum x2 -> x0, waiting for transfers between devices: 68.5 us -> none  [project(): return lax.psum(fold(fold(canvas, 'gx', 1, rim), 'gy', 2, rim), 'ma')]
    all_gather x0 -> x2, waiting for transfers between devices: none -> 53 us  [project(): lax.all_gather(fold(fold(canvas, 'gx', 1, rim), 'gy', 2, rim), 'ma')]
    ppermute x10, starting transfers between devices: 26.1 us -> 34.6 us  [shift_pair(): lax.ppermute(high_part, axis, forward)]
where the time goes in v1:
time: 386 us; the launch traced here: 384 us
  waiting for transfers between devices  142 us (37%)
  blocking collectives  78.9 us (20%)
  starting transfers between devices  47.5 us (12%)
  other arithmetic  39.4 us (10%)
  between operations  32.3 us (8%)
  matrix products  23.1 us (6%)
  local copies, waits for them, and re-layouts  21.2 us (5%)
    psum x2, blocking collectives, shards(): sums = lax.psum(sums, ('gx', 'gy', 'ma'))  78.9 us
    all_gather x2, waiting for transfers between devices, project(): lax.all_gather(fold(fold(canvas, 'gx', 1, rim), 'gy', 2, rim), 'ma')  53 us
    all_gather x1, waiting for transfers between devices, shards(): probes = lax.all_gather(probe_shard, 'ma', axis=0, tiled=True)  52.5 us
    ppermute x10, starting transfers between devices, shift_pair(): lax.ppermute(high_part, axis, forward)  34.6 us
    ppermute x10, waiting for transfers between devices, shift_pair(): lax.ppermute(low_part, axis, backward)  27.2 us
    dot_general x3, matrix products, spectra_of(): jnp.einsum('smcik,ckl->smil', halfway, right_two, preferred_element_type=...  16 us
    ppermute x10, starting transfers between devices, shift_pair(): lax.ppermute(low_part, axis, backward)  12.9 us
    another operation x3, other arithmetic  11.5 us
  transfers between devices with their start and end apart: 23, of which 19 were waited for; matrix products, arithmetic and copies ran while one was open for 1% of the time, Pallas kernels for 0%

profile of v1, /device:TPU:0, one launch (start us, length us, event | category | flops | bytes accessed | tf_op | source)
XLA Modules:
  0.0 384.3 jit_solution(9204904624788202651)
XLA Ops:
  7.3 1.0 fusion.79
  8.3 4.9 %collective-permute-start = (f32[2,128,128]{2,1,0:T(8,128)S(1)}, f32[2,128,128]{2,1,0:T(8,128)S(1)}, u32[]{:S(2)}, u32[]{:S(2)}) collective-permute-start(f32[2,128,128]{2,1,0:T(8,128)S(1)} %get-tuple-element.52), channel_id=1, source_target_pairs={{0,4},{4,8},{8,12},{1,5},{5,9},{9,13},{2,6},{6,10},{10,14},{3,7},{... | collective-permute-start | bytes 393224 | tf_op jit(solution)/shard_map/ppermute | solution.py:27
  13.2 1.3 collective-permute-start.1
  14.5 1.4 collective-permute-done
  16.9 3.8 collective-permute-done.1
  20.7 1.3 collective-permute-start.3
  22.0 3.1 collective-permute-start.2
  39.9 52.5 %all-gather.6.cloned.1.call-done = f32[8,2,256,256]{3,2,1,0:T(8,128)} async-done(((f32[2,2,256,256]{3,2,1,0:T(8,128)}), f32[8,2,256,256]{3,2,1,0:T(8,128)}) %all-gather.6.cloned.1.call-update) | async-done | bytes 4194320 | tf_op jit(solution)/shard_map/all_gather | solution.py:71
  92.4 4.0 %slice_bitcast_fusion.5 = (f32[8,256,256]{2,1,0:T(8,128)S(1)}, f32[8,256,256]{2,1,0:T(8,128)}) fusion(f32[8,2,256,256]{3,2,1,0:T(8,128)} %all-gather.6.cloned.1.call-done), kind=kLoop, calls=%fused_computation.38 | loop fusion | bytes 8388608 | tf_op jit(solution)/shard_map/mul | solution.py:108
  96.4 1.8 copy.22
  98.2 2.9 copy.25
  101.1 4.8 %subtract_convert_fusion.2 = (bf16[2,8,1,256,256]{4,3,2,1,0:T(8,128)(2,1)}, bf16[2,8,1,256,256]{4,3,2,1,0:T(8,128)(2,1)}) fusion(f32[2,256,256]{2,1,0:T(8,128)S(1)} %get-tuple-element.38, f32[8,256,256]{2,1,0:T(8,128)} %get-tuple-element.22, f32[2,256,256]{2,1,0:T(8,128)S(1)} %get-tuple-element.37, f32[8,256,256]{2,1,0:T(8,128)S(1)} %get-tuple-element.21), kind=kLoop, calls=%fused_computation.34 | loop fusion | flops 8388608 | bytes 9437184 | tf_op jit(solution)/shard_map/convert.4
  105.8 5.6 %bitcast_multiply_fusion.4 = (f32[2,8,64,512]{3,2,1,0:T(8,128)}, f32[2,8,64,512,1]{3,2,4,1,0:T(8,128)}) fusion(bf16[2,256,512,1,1]{2,1,0,4,3:T(8,128)(2,1)} %constant.64, bf16[2,8,1,256,256]{4,3,2,1,0:T(8,128)(2,1)} %get-tuple-element.20, bf16[2,8,1,256,256]{4,3,2,1,0:T(8,128)(2,1)} %get-tuple-element.19, bf16[2,256,2,256]{3,1,2,0:T(8,128)(2,1)} %constant.61, ...), kind=kOutput, calls=%fused_computation.46 | convolution fusion | flops 1083179008 | bytes 9043972 | tf_op jit(solution)/shard_map/smcik,ckl->smil/dot_general | solution.py:90
  111.4 1.8 fusion.24
  113.3 1.0 fusion.53
  114.3 1.8 convolution_convert_fusion.1
  116.1 1.3 reshape.91
  117.4 2.3 convolution_bitcast_fusion.1
  119.8 1.6 add_reduce_fusion.1
  123.9 1.6 collective-permute-start.4
  125.6 1.3 collective-permute-start.5
  127.0 2.3 collective-permute-done.5
  129.5 3.4 collective-permute-start.6
  132.9 1.3 collective-permute-start.7
  134.2 1.7 collective-permute-done.6
  135.9 4.7 %collective-permute-done.7 = f32[2,128,128]{1,2,0:T(8,128)S(1)} collective-permute-done((f32[2,128,128]{1,2,0:T(8,128)S(1)}, f32[2,128,128]{1,2,0:T(8,128)S(1)}, u32[]{:S(2)}, u32[]{:S(2)}) %collective-permute-start.7) | collective-permute-done | bytes 131104 | tf_op jit(solution)/shard_map/ppermute | solution.py:27
  141.6 26.1 %all-gather.8.cloned.1.call-done = f32[8,128,256]{2,1,0:T(8,128)} async-done(((f32[2,128,256]{2,1,0:T(8,128)}), f32[8,128,256]{2,1,0:T(8,128)}) %all-gather.8.cloned.1.call-update) | async-done | bytes 1048592 | tf_op jit(solution)/shard_map/all_gather | solution.py:117
  167.8 1.3 reduce_sum.129
  169.8 3.4 collective-permute-start.8
  173.2 1.3 collective-permute-start.9
  174.5 1.2 collective-permute-done.8
  175.7 4.7 %collective-permute-done.9 = f32[2,128,128]{2,1,0:T(8,128)S(1)} collective-permute-done((f32[2,128,128]{2,1,0:T(8,128)S(1)}, f32[2,128,128]{2,1,0:T(8,128)S(1)}, u32[]{:S(2)}, u32[]{:S(2)}) %collective-permute-start.9) | collective-permute-done | bytes 131104 | tf_op jit(solution)/shard_map/ppermute | solution.py:27
  180.4 1.3 collective-permute-start.11
  181.7 4.7 %collective-permute-start.10 = (f32[2,128,512]{2,1,0:T(8,128)S(1)}, f32[2,128,512]{2,1,0:T(8,128)}, u32[]{:S(2)}, u32[]{:S(2)}) collective-permute-start(f32[2,128,512]{2,1,0:T(8,128)S(1)} %pad_maximum_fusion.6), channel_id=1, source_target_pairs={{0,16},{1,17},{2,18},{3,19},{4,20},{5,21},{6,22},{7,23},{8,24},{9,... | collective-permute-start | bytes 1572872 | tf_op jit(solution)/shard_map/ppermute | solution.py:27
  187.2 1.3 pad_maximum_fusion.1
  189.1 1.1 copy-done
  190.2 3.4 subtract_convert_fusion.1
  193.6 6.2 %bitcast_multiply_fusion.2 = (f32[2,8,64,512]{3,2,1,0:T(8,128)}, f32[2,8,64,512,1]{3,2,4,1,0:T(8,128)}) fusion(f32[2,8,64,512,1]{3,2,4,1,0:T(8,128)} %get-tuple-element.62, bf16[2,256,512,1,1]{2,1,0,4,3:T(8,128)(2,1)S(1)} %copy-done.11, bf16[2,8,1,256,256]{4,3,2,1,0:T(8,128)(2,1)} %get-tuple-element.18, bf16[2,8,1,256,256]{4,3,2,1,0:T(8,128)(2,1)} %get-tuple-element.17, ...), kind=kOutput, calls=%fused_computation.42 | convolution fusion | flops 1083179008 | bytes 11141124 | tf_op jit(solution)/shard_map/smcik,ckl->smil/dot_general | solution.py:90
  199.8 1.7 fusion.23
  202.9 39.5 %psum.14 = f32[2]{0:T(128)S(1)} all-reduce(f32[2]{0:T(128)S(1)} %pad_maximum_fusion.8), channel_id=1, replica_groups=mesh['gx'=2,'gy'=4,'ma'=4] {'gx','gy','ma'}, use_global_device_ids=true, to_apply=%region_7.8 | all-reduce | flops 2 | bytes 16 | tf_op jit(solution)/shard_map/psum | solution.py:129
  244.9 3.0 fusion.69
  248.0 1.5 fusion.54
  250.4 2.3 convolution_bitcast_fusion
  252.7 1.6 add_reduce_fusion
  256.9 1.3 collective-permute-start.12
  258.2 1.3 collective-permute-start.13
  259.7 2.3 collective-permute-done.13
  262.1 4.2 %collective-permute-start.14 = (f32[2,128,128]{1,2,0:T(8,128)S(1)}, f32[2,128,128]{1,2,0:T(8,128)S(1)}, u32[]{:S(2)}, u32[]{:S(2)}) collective-permute-start(f32[2,128,128]{1,2,0:T(8,128)S(1)} %get-tuple-element.39), channel_id=1, source_target_pairs={{0,4},{4,8},{8,12},{1,5},{5,9},{9,13},{2,6},{6,10},{10,14},{3,7},{... | collective-permute-start | bytes 393224 | tf_op jit(solution)/shard_map/ppermute | solution.py:27
  266.3 1.3 collective-permute-start.15
  267.6 1.7 collective-permute-done.14
  269.4 4.7 %collective-permute-done.15 = f32[2,128,128]{1,2,0:T(8,128)S(1)} collective-permute-done((f32[2,128,128]{1,2,0:T(8,128)S(1)}, f32[2,128,128]{1,2,0:T(8,128)S(1)}, u32[]{:S(2)}, u32[]{:S(2)}) %collective-permute-start.15) | collective-permute-done | bytes 131104 | tf_op jit(solution)/shard_map/ppermute | solution.py:27
  275.0 26.9 %all-gather.10.cloned.1.call-done = f32[8,128,256]{2,1,0:T(8,128)} async-done(((f32[2,128,256]{2,1,0:T(8,128)}), f32[8,128,256]{2,1,0:T(8,128)}) %all-gather.10.cloned.1.call-update) | async-done | bytes 1048592 | tf_op jit(solution)/shard_map/all_gather | solution.py:117
  301.9 1.3 reduce_sum.136
  304.0 3.4 collective-permute-start.16
  307.4 1.3 collective-permute-start.17
  308.7 1.2 collective-permute-done.16
  309.9 4.7 %collective-permute-done.17 = f32[2,128,128]{2,1,0:T(8,128)S(1)} collective-permute-done((f32[2,128,128]{2,1,0:T(8,128)S(1)}, f32[2,128,128]{2,1,0:T(8,128)S(1)}, u32[]{:S(2)}, u32[]{:S(2)}) %collective-permute-start.17) | collective-permute-done | bytes 131104 | tf_op jit(solution)/shard_map/ppermute | solution.py:27
  316.1 1.3 collective-permute-start.19
  317.4 4.6 %collective-permute-start.18 = (f32[2,128,512]{2,1,0:T(8,128)}, f32[2,128,512]{2,1,0:T(8,128)}, u32[]{:S(2)}, u32[]{:S(2)}) collective-permute-start(f32[2,128,512]{2,1,0:T(8,128)} %pad_maximum_fusion.7), channel_id=1, source_target_pairs={{0,16},{1,17},{2,18},{3,19},{4,20},{5,21},{6,22},{7,23},{8,24},{9,... | collective-permute-start | bytes 1572872 | tf_op jit(solution)/shard_map/ppermute | solution.py:27
  323.0 1.4 pad_maximum_fusion.2
  324.9 1.1 copy-done.1
  326.0 3.3 subtract_convert_fusion
  329.3 4.2 %bitcast_multiply_fusion = f32[2,8,64,512]{3,2,1,0:T(8,128)S(1)} fusion(f32[2,8,64,512]{3,2,1,0:T(8,128)} %copy-done.7, bf16[2,256,512,1,1]{2,1,0,4,3:T(8,128)(2,1)S(1)} %copy-done.11, bf16[2,8,1,256,256]{4,3,2,1,0:T(8,128)(2,1)} %get-tuple-element.16, bf16[2,8,1,256,256]{4,3,2,1,0:T(8,128)(2,1)} %get-tuple-element.15, ...), kind=kOutput, calls=%fused_computation.39 | convolution fusion | flops 1083179008 | bytes 9043972 | tf_op jit(solution)/shard_map/smcik,ckl->smil/dot_general | solution.py:90
  335.1 39.5 %psum.15 = f32[2]{0:T(128)S(1)} all-reduce(f32[2]{0:T(128)S(1)} %pad_maximum_fusion.9), channel_id=1, replica_groups=mesh['gx'=2,'gy'=4,'ma'=4] {'gx','gy','ma'}, use_global_device_ids=true, to_apply=%region_15.16 | all-reduce | flops 2 | bytes 16 | tf_op jit(solution)/shard_map/psum | solution.py:129
  (87 shorter events, 20.8 us)
Async XLA Ops:
  6.5 18.6 %copy-start.13 = (s32[1,1,2,2]{3,2,1,0:T(2,128)S(1)}, s32[1,1,2,2]{3,2,1,0:T(2,128)}, u32[]{:S(2)}) copy-start(s32[1,1,2,2]{3,2,1,0:T(2,128)} %param.10) | copy-start | bytes 52
  6.5 85.9 %all-gather.6.cloned.1.call-start = ((), (), s32[]{:S(2)}) async-start(), calls=%async_computation | async-start | bytes 5242880 | tf_op jit(solution)/shard_map/all_gather | solution.py:71
  7.3 160.5 %all-gather.8.cloned.1.call-start = ((), (), s32[]{:S(2)}) async-start(), calls=%async_computation.1 | async-start | bytes 1310720 | tf_op jit(solution)/shard_map/all_gather | solution.py:117
  8.3 7.6 %collective-permute-start = (f32[2,128,128]{2,1,0:T(8,128)S(1)}, f32[2,128,128]{2,1,0:T(8,128)S(1)}, u32[]{:S(2)}, u32[]{:S(2)}) collective-permute-start(f32[2,128,128]{2,1,0:T(8,128)S(1)} %get-tuple-element.52), channel_id=1, source_target_pairs={{0,4},{4,8},{8,12},{1,5},{5,9},{9,13},{2,6},{6,10},{10,14},{3,7},{... | collective-permute-start | bytes 393224 | tf_op jit(solution)/shard_map/ppermute | solution.py:27
  13.2 7.5 %collective-permute-start.1 = (f32[2,128,128]{2,1,0:T(8,128)S(1)}, f32[2,128,128]{2,1,0:T(8,128)S(1)}, u32[]{:S(2)}, u32[]{:S(2)}) collective-permute-start(f32[2,128,128]{2,1,0:T(8,128)S(1)} %get-tuple-element.51), channel_id=1, source_target_pairs={{4,0},{8,4},{12,8},{5,1},{9,5},{13,9},{6,2},{10,6},{14,10},{7,3},{... | collective-permute-start | bytes 393224 | tf_op jit(solution)/shard_map/ppermute | solution.py:27
  20.7 18.6 %collective-permute-start.3 = (f32[2,128,512]{2,1,0:T(8,128)S(1)}, f32[2,128,512]{2,1,0:T(8,128)S(1)}, u32[]{:S(2)}, u32[]{:S(2)}) collective-permute-start(f32[2,128,512]{2,1,0:T(8,128)S(1)} %constant_dynamic-update-slice_fusion), channel_id=1, source_target_pairs={{16,0},{17,1},{18,2},{19,3},{20,4},{21,5},{22,6},{23,7},{24,8},{25... | collective-permute-start | bytes 1572872 | tf_op jit(solution)/shard_map/ppermute | solution.py:27
  22.0 17.3 %collective-permute-start.2 = (f32[2,128,512]{2,1,0:T(8,128)S(1)}, f32[2,128,512]{2,1,0:T(8,128)S(1)}, u32[]{:S(2)}, u32[]{:S(2)}) collective-permute-start(f32[2,128,512]{2,1,0:T(8,128)S(1)} %constant_dynamic-update-slice_fusion), channel_id=1, source_target_pairs={{0,16},{1,17},{2,18},{3,19},{4,20},{5,21},{6,22},{7,23},{8,24},{9,... | collective-permute-start | bytes 1572872 | tf_op jit(solution)/shard_map/ppermute | solution.py:27
  111.4 2.9 copy-start.6
  111.4 2.9 copy-start.9
  117.4 2.4 copy-start.2
  117.4 2.4 copy-start.4
  123.9 3.1 collective-permute-start.4
  125.6 3.8 collective-permute-start.5
  129.5 6.4 %collective-permute-start.6 = (f32[2,128,128]{1,2,0:T(8,128)S(1)}, f32[2,128,128]{1,2,0:T(8,128)S(1)}, u32[]{:S(2)}, u32[]{:S(2)}) collective-permute-start(f32[2,128,128]{1,2,0:T(8,128)S(1)} %get-tuple-element.41), channel_id=1, source_target_pairs={{0,4},{4,8},{8,12},{1,5},{5,9},{9,13},{2,6},{6,10},{10,14},{3,7},{... | collective-permute-start | bytes 393224 | tf_op jit(solution)/shard_map/ppermute | solution.py:27
  132.9 7.8 %collective-permute-start.7 = (f32[2,128,128]{1,2,0:T(8,128)S(1)}, f32[2,128,128]{1,2,0:T(8,128)S(1)}, u32[]{:S(2)}, u32[]{:S(2)}) collective-permute-start(f32[2,128,128]{1,2,0:T(8,128)S(1)} %get-tuple-element.42), channel_id=1, source_target_pairs={{4,0},{8,4},{12,8},{5,1},{9,5},{13,9},{6,2},{10,6},{14,10},{7,3},{... | collective-permute-start | bytes 393224 | tf_op jit(solution)/shard_map/ppermute | solution.py:27
  141.6 160.3 %all-gather.10.cloned.1.call-start = ((), (), s32[]{:S(2)}) async-start(), calls=%async_computation.2 | async-start | bytes 1310720 | tf_op jit(solution)/shard_map/all_gather | solution.py:117
  169.8 5.9 %collective-permute-start.8 = (f32[2,128,128]{2,1,0:T(8,128)S(1)}, f32[2,128,128]{2,1,0:T(8,128)S(1)}, u32[]{:S(2)}, u32[]{:S(2)}) collective-permute-start(f32[2,128,128]{2,1,0:T(8,128)S(1)} %get-tuple-element.49), channel_id=1, source_target_pairs={{0,4},{4,8},{8,12},{1,5},{5,9},{9,13},{2,6},{6,10},{10,14},{3,7},{... | collective-permute-start | bytes 393224 | tf_op jit(solution)/shard_map/ppermute | solution.py:27
  173.2 7.2 %collective-permute-start.9 = (f32[2,128,128]{2,1,0:T(8,128)S(1)}, f32[2,128,128]{2,1,0:T(8,128)S(1)}, u32[]{:S(2)}, u32[]{:S(2)}) collective-permute-start(f32[2,128,128]{2,1,0:T(8,128)S(1)} %get-tuple-element.50), channel_id=1, source_target_pairs={{4,0},{8,4},{12,8},{5,1},{9,5},{13,9},{6,2},{10,6},{14,10},{7,3},{... | collective-permute-start | bytes 393224 | tf_op jit(solution)/shard_map/ppermute | solution.py:27
  180.4 6.6 %collective-permute-start.11 = (f32[2,128,512]{2,1,0:T(8,128)S(1)}, f32[2,128,512]{2,1,0:T(8,128)}, u32[]{:S(2)}, u32[]{:S(2)}) collective-permute-start(f32[2,128,512]{2,1,0:T(8,128)S(1)} %pad_maximum_fusion.6), channel_id=1, source_target_pairs={{16,0},{17,1},{18,2},{19,3},{20,4},{21,5},{22,6},{23,7},{24,8},{25... | collective-permute-start | bytes 1572872 | tf_op jit(solution)/shard_map/ppermute | solution.py:27
  181.7 5.5 %collective-permute-start.10 = (f32[2,128,512]{2,1,0:T(8,128)S(1)}, f32[2,128,512]{2,1,0:T(8,128)}, u32[]{:S(2)}, u32[]{:S(2)}) collective-permute-start(f32[2,128,512]{2,1,0:T(8,128)S(1)} %pad_maximum_fusion.6), channel_id=1, source_target_pairs={{0,16},{1,17},{2,18},{3,19},{4,20},{5,21},{6,22},{7,23},{8,24},{9,... | collective-permute-start | bytes 1572872 | tf_op jit(solution)/shard_map/ppermute | solution.py:27
  188.6 1.6 copy-start
  190.2 3.4 copy-start.11
  247.9 2.5 copy-start.7
  247.9 1.7 copy-start.10
  250.4 2.4 copy-start.3
  250.4 2.4 copy-start.5
  256.9 2.8 collective-permute-start.12
  258.2 3.8 collective-permute-start.13
  262.1 7.2 %collective-permute-start.14 = (f32[2,128,128]{1,2,0:T(8,128)S(1)}, f32[2,128,128]{1,2,0:T(8,128)S(1)}, u32[]{:S(2)}, u32[]{:S(2)}) collective-permute-start(f32[2,128,128]{1,2,0:T(8,128)S(1)} %get-tuple-element.39), channel_id=1, source_target_pairs={{0,4},{4,8},{8,12},{1,5},{5,9},{9,13},{2,6},{6,10},{10,14},{3,7},{... | collective-permute-start | bytes 393224 | tf_op jit(solution)/shard_map/ppermute | solution.py:27
  266.3 7.7 %collective-permute-start.15 = (f32[2,128,128]{1,2,0:T(8,128)S(1)}, f32[2,128,128]{1,2,0:T(8,128)S(1)}, u32[]{:S(2)}, u32[]{:S(2)}) collective-permute-start(f32[2,128,128]{1,2,0:T(8,128)S(1)} %get-tuple-element.40), channel_id=1, source_target_pairs={{4,0},{8,4},{12,8},{5,1},{9,5},{13,9},{6,2},{10,6},{14,10},{7,3},{... | collective-permute-start | bytes 393224 | tf_op jit(solution)/shard_map/ppermute | solution.py:27
  304.0 5.9 %collective-permute-start.16 = (f32[2,128,128]{2,1,0:T(8,128)S(1)}, f32[2,128,128]{2,1,0:T(8,128)S(1)}, u32[]{:S(2)}, u32[]{:S(2)}) collective-permute-start(f32[2,128,128]{2,1,0:T(8,128)S(1)} %get-tuple-element.45), channel_id=1, source_target_pairs={{0,4},{4,8},{8,12},{1,5},{5,9},{9,13},{2,6},{6,10},{10,14},{3,7},{... | collective-permute-start | bytes 393224 | tf_op jit(solution)/shard_map/ppermute | solution.py:27
  307.4 7.2 %collective-permute-start.17 = (f32[2,128,128]{2,1,0:T(8,128)S(1)}, f32[2,128,128]{2,1,0:T(8,128)S(1)}, u32[]{:S(2)}, u32[]{:S(2)}) collective-permute-start(f32[2,128,128]{2,1,0:T(8,128)S(1)} %get-tuple-element.46), channel_id=1, source_target_pairs={{4,0},{8,4},{12,8},{5,1},{9,5},{13,9},{6,2},{10,6},{14,10},{7,3},{... | collective-permute-start | bytes 393224 | tf_op jit(solution)/shard_map/ppermute | solution.py:27
  314.5 0.7 copy-start.12
  316.1 6.5 %collective-permute-start.19 = (f32[2,128,512]{2,1,0:T(8,128)}, f32[2,128,512]{2,1,0:T(8,128)}, u32[]{:S(2)}, u32[]{:S(2)}) collective-permute-start(f32[2,128,512]{2,1,0:T(8,128)} %pad_maximum_fusion.7), channel_id=1, source_target_pairs={{16,0},{17,1},{18,2},{19,3},{20,4},{21,5},{22,6},{23,7},{24,8},{25... | collective-permute-start | bytes 1572872 | tf_op jit(solution)/shard_map/ppermute | solution.py:27
  317.4 5.7 %collective-permute-start.18 = (f32[2,128,512]{2,1,0:T(8,128)}, f32[2,128,512]{2,1,0:T(8,128)}, u32[]{:S(2)}, u32[]{:S(2)}) collective-permute-start(f32[2,128,512]{2,1,0:T(8,128)} %pad_maximum_fusion.7), channel_id=1, source_target_pairs={{0,16},{1,17},{2,18},{3,19},{4,20},{5,21},{6,22},{7,23},{8,24},{9,... | collective-permute-start | bytes 1572872 | tf_op jit(solution)/shard_map/ppermute | solution.py:27
  324.4 1.6 copy-start.1
  333.5 43.5 %copy-start.8 = (f32[2,128,256]{2,1,0:T(8,128)S(1)}, f32[2,128,256]{2,1,0:T(8,128)}, u32[]{:S(2)}) copy-start(f32[2,128,256]{2,1,0:T(8,128)} %param.7) | copy-start | bytes 786436
Sparse Core Ops, SparseCore 0:
  8.9 83.4 all-gather.5
  141.7 26.0 all-gather.7
  275.1 26.7 all-gather.9
